TPU v7x, 32 devices: a whole 2x2x4 slice. The times are simulated.
32 devices in a mesh: expert: 2 (over x), tensor: 16 (over z, y, core).
Axes of the slice: x: 2, y: 2, z: 4, core: 2. Of those that a mesh axis runs over, the one named last changes fastest.
Arguments:
- tokens: bfloat16 [96, 6144], P('expert', 'tensor'), may hold values from -6 to 6
- expert_ids: int32 [96, 2], P('expert'), may hold values from 0 to 1, as said below
- route_weight: int32 [96, 2], P('expert'), may hold values from 1 to 4095
- gate_weight: bfloat16 [2, 6144, 8192], P('expert', None, 'tensor'), may hold values from -0.078125 to 0.078125
- up_weight: bfloat16 [2, 6144, 8192], P('expert', None, 'tensor'), may hold values from -0.078125 to 0.078125
- down_weight: bfloat16 [2, 8192, 6144], P('expert', 'tensor'), may hold values from -0.0625 to 0.0625
Outputs:
- mixed: bfloat16 [96, 6144], P('expert', 'tensor')
- expert_load: float32 [2, 2], replicated
Inputs may be any that keep to these rules, and one draw needn't show every extreme that they name: `expert_ids`: each row names two different experts. The hot expert is the one named in the first column of the first row of every aligned block of 48 rows (the tokens of one expert group), the same in all blocks. In each block exactly 48 rows name the hot expert, in either column; every other expert is named by 7 or 48 rows of each block, and by exactly 48 rows in some.
All inputs are finite; a program needn't handle non-finite values.
Results may differ from a plain program's by a relative error of at most 0.005.
Values may be sent and summed in bfloat16 or wider, within the bound.
A program may use at most 64 MiB of HBM per device.

v0:
```python
import functools

import jax
import jax.numpy as jnp
from jax import lax
from jax.experimental import pallas as pl
from jax.experimental.pallas import tpu as pltpu
from jax.sharding import PartitionSpec as P

MESH = pl.DeviceIdType.MESH
LANES = 128


def near_first(step, count):
    return ((step + 1) // 2) * (2 * (step % 2) - 1) + count


def kernel(
    depth,
    tok_ref, ids_ref, raw_ref, gate_hbm, up_hbm, down_hbm,
    out_ref, load_ref,
    tok_all, gate_buf, up_buf, down_buf, gate_acc, up_acc, hidden,
    keep, pair_out, pair_in, rs_out, in_one, out_two, in_two, out_three, in_three,
    ids_in, raw_in, mix,
    gate_sem, up_sem, down_sem, own_sem,
    z_send, one_send, two_send, sib_send, ag_recv,
    pair_send, pair_recv, rs_one_send, rs_one_recv, rs_two_send, rs_two_recv, rs_z_send, rs_z_recv,
    st_send, st_recv,
):
    rows, width = tok_ref.shape
    wide = 2 * width
    e = lax.axis_index("expert")
    t = lax.axis_index("tensor")
    c = t % 2
    y = (t // 2) % 2
    z = t // 4
    e_one, y_one = e + (1 - c) * (1 - 2 * e), y + c * (1 - 2 * y)
    e_two, y_two = e + c * (1 - 2 * e), y + (1 - c) * (1 - 2 * y)
    lines = ((e, y), (e_one, y_one), (e_two, y_two), (1 - e, 1 - y))

    def device(e2, z2, y2, c2):
        return (e2, 4 * z2 + 2 * y2 + c2)

    first = device(e_one, z, y_one, c)
    second = device(e_two, z, y_two, c)
    sibling = device(e, z, y, 1 - c)
    across = device(1 - e, z, y, c)

    def z_at(step):
        return (z + near_first(step, depth)) % depth

    def chip(z2, y2):
        return 2 * z2 + y2

    def row_span(e2):
        return pl.ds(pl.multiple_of(e2 * rows, 16), rows)

    def weight_copies(m):
        span = pl.ds(pl.multiple_of(m * wide, LANES), wide)
        return (
            pltpu.make_async_copy(gate_hbm.at[0, span, :], gate_buf.at[m], gate_sem.at[m]),
            pltpu.make_async_copy(up_hbm.at[0, span, :], up_buf.at[m], up_sem.at[m]),
        )

    def down_copy(m):
        span = pl.ds(pl.multiple_of(m * wide, LANES), wide)
        return pltpu.make_async_copy(down_hbm.at[0, :, span], down_buf.at[m], down_sem.at[m])

    def slot(e2, z2, y2, parity):
        lanes = pl.ds(pl.multiple_of(parity * width, LANES), width)
        return tok_all.at[chip(z2, y2), row_span(e2), lanes]

    for y2 in (y, 1 - y):
        for step in range(depth):
            for copy in weight_copies(chip(z_at(step), y2)):
                copy.start()
    for step in range(depth):
        for y2 in (1 - y, y):
            down_copy(chip(z_at(depth - 1 - step), y2)).start()

    own_copy = pltpu.make_async_copy(tok_ref, slot(e, z, y, c), own_sem)
    own_copy.start()

    barrier = pltpu.get_barrier_semaphore()
    friends = [sibling, first, second]
    friends += [device(e, z_at(step), y, c) for step in range(1, depth)]
    for friend in friends:
        pl.semaphore_signal(barrier, inc=1, device_id=friend, device_id_type=MESH)
    pl.semaphore_wait(barrier, len(friends))

    def remote(src, dst, send, recv, target):
        return pltpu.make_async_remote_copy(
            src_ref=src, dst_ref=dst, send_sem=send, recv_sem=recv,
            device_id=target, device_id_type=MESH,
        )

    def token_copy(source, e2, z2, y2, send, target):
        place = slot(e2, z2, y2, c)
        arrived = ag_recv.at[e2, 4 * z2 + 2 * y2 + c]
        return remote(place if source is None else source, place, send, arrived, target)

    def spread(line, step, source=None):
        e2, y2 = lines[line]
        z2 = z_at(step)
        copies = []
        if line == 0:
            copies.append(token_copy(source, e2, z2, y2, one_send.at[step], first))
        if line <= 1:
            copies.append(token_copy(source, e2, z2, y2, two_send.at[line, step], second))
        copies.append(token_copy(source, e2, z2, y2, sib_send.at[line, step], sibling))
        return copies

    def z_copy(step):
        return token_copy(tok_ref, e, z, y, z_send.at[step], device(e, z_at(step), y, c))

    def token_wait(e2, z2, y2, parity):
        place = slot(e2, z2, y2, parity)
        remote(place, place, own_sem, ag_recv.at[e2, 4 * z2 + 2 * y2 + parity], sibling).wait_recv()

    def stat_copies():
        return (
            remote(ids_ref, ids_in, st_send.at[0], st_recv.at[0], across),
            remote(raw_ref, raw_in, st_send.at[1], st_recv.at[1], across),
        )

    for step in range(1, depth):
        z_copy(step).start()
    for copy in spread(0, 0, tok_ref):
        copy.start()
    for copy in stat_copies():
        copy.start()

    gate_acc[...] = jnp.zeros_like(gate_acc)
    up_acc[...] = jnp.zeros_like(up_acc)
    own_copy.wait()

    for line in range(3):
        for step in range(depth):
            if (line, step) == (0, 0):
                continue
            e2, y2 = lines[line]
            token_wait(e2, z_at(step), y2, c)
            for copy in spread(line, step):
                copy.start()

    for copy in stat_copies():
        copy.wait_recv()
    held = []
    for ids_part, raw_part in ((ids_ref, raw_ref), (ids_in, raw_in)):
        ids = ids_part[...]
        raw = raw_part[...].astype(jnp.float32)
        held.append((ids, raw / jnp.sum(raw, axis=0, keepdims=True)))
    square = (rows, rows)
    diagonal = lax.broadcasted_iota(jnp.int32, square, 0) == lax.broadcasted_iota(jnp.int32, square, 1)
    for (ids, share), e2 in zip(held, (e, 1 - e)):
        line_mix = jnp.sum(jnp.where(ids == e, share, 0.0), axis=0, keepdims=True)
        column = jnp.sum(jnp.where(diagonal, line_mix, 0.0), axis=1, keepdims=True)
        mix[row_span(e2), :] = jnp.broadcast_to(column, (rows, LANES))
    row_at = lax.broadcasted_iota(jnp.int32, (2, 2), 0)
    lane_at = lax.broadcasted_iota(jnp.int32, (2, 2), 1)
    load = jnp.zeros((2, 2), jnp.float32)
    for label in range(2):
        counts, weights = [], []
        for ids, share in held:
            hit = ids == label
            counts.append(jnp.sum(hit.astype(jnp.float32), axis=(0, 1), keepdims=True))
            weights.append(jnp.sum(jnp.where(hit, share, 0.0), axis=(0, 1), keepdims=True))
        load = jnp.where((lane_at == label) & (row_at == 0), counts[0] + counts[1], load)
        load = jnp.where((lane_at == label) & (row_at == 1), weights[0] + weights[1], load)
    load_ref[...] = load / rows

    def first_layer(m):
        for copy in weight_copies(m):
            copy.wait()
        left = tok_all[m]
        gate_acc[...] += jnp.dot(left, gate_buf[m], preferred_element_type=jnp.float32)
        up_acc[...] += jnp.dot(left, up_buf[m], preferred_element_type=jnp.float32)

    def last_blocks(step):
        e2, y2 = lines[3]
        token_wait(e2, z_at(step), y2, c)
        for copy in spread(3, step):
            copy.start()

    @pl.loop(0, depth)
    def _(step):
        last_blocks(step)
        for e2 in (e, 1 - e):
            token_wait(e2, z_at(step), y, 1 - c)
        first_layer(chip(z_at(step), y))

    @pl.loop(0, depth)
    def _(step):
        for e2 in (e, 1 - e):
            token_wait(e2, z_at(step), 1 - y, 1 - c)
        first_layer(chip(z_at(step), 1 - y))

    gate = gate_acc[...]
    hidden[...] = (gate / (1.0 + jnp.exp(-gate)) * up_acc[...]).astype(hidden.dtype)

    def pair_copy(m):
        return remote(pair_out.at[m], pair_in.at[m], pair_send.at[m], pair_recv.at[m], sibling)

    def send_one(line, z2):
        e2, y2 = lines[line]
        return remote(
            rs_out.at[chip(z2, y2), row_span(e2)], in_one.at[line - 2, z2],
            rs_one_send.at[line - 2, z2], rs_one_recv.at[line - 2, z2], second,
        )

    def send_two(z2):
        return remote(out_two.at[z2], in_two.at[z2], rs_two_send.at[z2], rs_two_recv.at[z2], first)

    def send_three(z2):
        target = device(e, z2, y, c)
        return remote(out_three.at[z2], in_three.at[z], rs_z_send.at[z2], rs_z_recv.at[z], target)

    def second_layer(m):
        down_copy(m).wait()
        part = jnp.dot(hidden[...], down_buf[m], preferred_element_type=jnp.float32)
        part = part * mix[:, :1]
        low, high = part[:, :width], part[:, width:]
        pair_out[m] = jnp.where(c == 0, high, low).astype(pair_out.dtype)
        keep[m] = jnp.where(c == 0, low, high)
        pair_copy(m).start()

    def join_pair(z2):
        for y2 in (1 - y, y):
            m = chip(z2, y2)
            pair_copy(m).wait_recv()
            total = keep[m] + pair_in[m].astype(jnp.float32)
            keep[m] = total
            rs_out[m] = total.astype(rs_out.dtype)
        send_one(3, z2).start()
        send_one(2, z2).start()

    def far(step):
        return z_at(depth - 1 - step)

    for y2 in (1 - y, y):
        second_layer(chip(far(0), y2))

    @pl.loop(1, depth)
    def _(step):
        for y2 in (1 - y, y):
            second_layer(chip(far(step), y2))
        join_pair(far(step - 1))

    join_pair(far(depth - 1))

    for step in range(depth):
        z2 = far(step)
        send_one(3, z2).wait_recv()
        total = keep[chip(z2, y_one), row_span(e_one)] + in_one[1, z2].astype(jnp.float32)
        out_two[z2] = total.astype(out_two.dtype)
        send_two(z2).start()
    for step in range(depth):
        z2 = far(step)
        send_one(2, z2).wait_recv()
        send_two(z2).wait_recv()
        total = keep[chip(z2, y), row_span(e)] + in_one[0, z2].astype(jnp.float32)
        total += in_two[z2].astype(jnp.float32)
        if step < depth - 1:
            out_three[z2] = total.astype(out_three.dtype)
            send_three(z2).start()
    for step in range(1, depth):
        z2 = z_at(step)
        remote(in_three.at[z2], in_three.at[z2], own_sem, rs_z_recv.at[z2], sibling).wait_recv()
        total += in_three[z2].astype(jnp.float32)
    out_ref[...] = total.astype(out_ref.dtype)

    for step in range(depth):
        if step > 0:
            z_copy(step).wait_send()
            send_three(z_at(step)).wait_send()
        for line in range(4):
            for copy in spread(line, step):
                copy.wait_send()
        for y2 in (y, 1 - y):
            pair_copy(chip(z_at(step), y2)).wait_send()
        send_one(2, z_at(step)).wait_send()
        send_one(3, z_at(step)).wait_send()
        send_two(z_at(step)).wait_send()
    for copy in stat_copies():
        copy.wait_send()


def fused(tokens, expert_ids, route_weight, gate_weight, up_weight, down_weight):
    groups, peers = lax.axis_size("expert"), lax.axis_size("tensor")
    rows, width = tokens.shape
    units = gate_weight.shape[2]
    depth, chips, wide, all_rows = peers // 4, peers // 2, 2 * width, groups * rows
    vmem = pl.BlockSpec(memory_space=pltpu.VMEM)
    anywhere = pl.BlockSpec(memory_space=pl.ANY)
    half, single, dma = jnp.bfloat16, jnp.float32, pltpu.SemaphoreType.DMA
    return pl.pallas_call(
        functools.partial(kernel, depth),
        out_shape=(
            jax.ShapeDtypeStruct((rows, width), half),
            jax.ShapeDtypeStruct((2, groups), single),
        ),
        in_specs=[vmem, vmem, vmem, anywhere, anywhere, anywhere],
        out_specs=(vmem, vmem),
        scratch_shapes=[
            pltpu.VMEM((chips, all_rows, wide), half),
            pltpu.VMEM((chips, wide, units), half),
            pltpu.VMEM((chips, wide, units), half),
            pltpu.VMEM((chips, units, wide), half),
            pltpu.VMEM((all_rows, units), single),
            pltpu.VMEM((all_rows, units), single),
            pltpu.VMEM((all_rows, units), half),
            pltpu.VMEM((chips, all_rows, width), single),
            pltpu.VMEM((chips, all_rows, width), half),
            pltpu.VMEM((chips, all_rows, width), half),
            pltpu.VMEM((chips, all_rows, width), half),
            pltpu.VMEM((2, depth, rows, width), half),
            pltpu.VMEM((depth, rows, width), half),
            pltpu.VMEM((depth, rows, width), half),
            pltpu.VMEM((depth, rows, width), half),
            pltpu.VMEM((depth, rows, width), half),
            pltpu.VMEM((2, rows), jnp.int32),
            pltpu.VMEM((2, rows), jnp.int32),
            pltpu.VMEM((all_rows, LANES), single),
            dma((chips,)), dma((chips,)), dma((chips,)), dma(()),
            dma((depth,)), dma((depth,)), dma((2, depth)), dma((4, depth)), dma((groups, peers)),
            dma((chips,)), dma((chips,)), dma((2, depth)), dma((2, depth)),
            dma((depth,)), dma((depth,)), dma((depth,)), dma((depth,)),
            dma((2,)), dma((2,)),
        ],
        compiler_params=pltpu.CompilerParams(
            collective_id=0, has_side_effects=True, vmem_limit_bytes=60 * 1024 * 1024
        ),
    )(tokens, expert_ids.T, route_weight.T, gate_weight, up_weight, down_weight)


def fits(mesh, tokens):
    groups, peers = mesh.shape["expert"], mesh.shape["tensor"]
    rows, width = tokens.shape[0] // groups, tokens.shape[1] // peers
    return groups == 2 and peers % 4 == 0 and rows % 16 == 0 and width % LANES == 0


def swiglu(gate_value, up_value):
    return (jax.nn.silu(gate_value) * up_value).astype(jnp.bfloat16)


def matmul(left, right):
    return jnp.dot(left, right, preferred_element_type=jnp.float32)


def route_stats(id_block, raw_block, labels):
    weights = raw_block.astype(jnp.float32)
    route_share = weights / jnp.sum(weights, axis=1, keepdims=True)
    flat_chosen = (
        (id_block[:, :, None] == labels[None, None, :])
        .astype(jnp.int32)
        .reshape(-1, labels.shape[0])
    )
    chosen_float = flat_chosen.astype(jnp.float32)
    stats = jnp.stack(
        [jnp.sum(chosen_float, axis=0), jnp.sum(route_share.reshape(-1, 1) * chosen_float, axis=0)]
    )
    return (route_share, flat_chosen, stats)


def hot_inputs(hot_local, hot_id, labels):
    is_target = (labels == hot_id)[:, None, None]
    send_rows = jnp.where(is_target, hot_local[None], jnp.zeros_like(hot_local)[None])
    arrived = lax.all_to_all(send_rows, "expert", split_axis=0, concat_axis=0, tiled=True)
    return arrived.reshape(-1, hot_local.shape[1])


def local(tokens, expert_ids, route_weight, gate_weight, up_weight, down_weight):
    tok_rows = expert_ids.shape[0]
    experts = lax.axis_size("expert") * gate_weight.shape[0]
    hot_rows = tok_rows - tok_rows // 8 * min(experts - 2, 1)
    capacity = (2 * tok_rows - hot_rows + experts - 2) // (experts - 1)
    hot_id = expert_ids[0, 0]
    own_gate = gate_weight[0]
    own_up = up_weight[0]
    own_down = down_weight[0]
    hot_gate_w, hot_up_w, hot_down_w = (own_gate, own_up, own_down)
    labels = jnp.arange(experts, dtype=jnp.int32)
    route_share, flat_chosen, local_stats = route_stats(expert_ids, route_weight, labels)
    cold_chosen = flat_chosen * (labels != hot_id).astype(jnp.int32)[None, :]
    slot_index = jnp.sum((jnp.cumsum(cold_chosen, axis=0) - 1) * cold_chosen, axis=1)
    is_live = jnp.sum(cold_chosen, axis=1)
    target = jnp.sum(cold_chosen * labels[None, :], axis=1) * capacity + slot_index
    buffer_rows = jnp.arange(experts * capacity, dtype=jnp.int32)
    cold_pick = ((target[None, :] == buffer_rows[:, None]) & (is_live[None, :] == 1)).astype(
        jnp.bfloat16
    )
    cold_pick = jnp.sum(cold_pick.reshape(experts * capacity, tok_rows, 2), axis=2)
    hot_match = (expert_ids == hot_id).astype(jnp.int32)
    hot_flag = jnp.sum(hot_match, axis=1)
    hot_rank = jnp.cumsum(hot_flag) - 1
    hot_slots = jnp.arange(hot_rows, dtype=jnp.int32)
    hot_pick = ((hot_rank[None, :] == hot_slots[:, None]) & (hot_flag[None, :] == 1)).astype(
        jnp.bfloat16
    )
    feature_width = tokens.shape[1]
    cold_send = (
        matmul(cold_pick, tokens).astype(jnp.bfloat16).reshape(experts, capacity, feature_width)
    )
    cold_recv = lax.all_to_all(
        cold_send, "expert", split_axis=0, concat_axis=0, tiled=True
    ).reshape(experts * capacity, feature_width)
    hot_input = hot_inputs(matmul(hot_pick, tokens).astype(jnp.bfloat16), hot_id, labels)
    cold_piece = lax.all_gather(cold_recv, "tensor", axis=1, tiled=True)
    hot_piece = lax.all_gather(hot_input, "tensor", axis=1, tiled=True)
    cold_gate = matmul(cold_piece, own_gate)
    cold_up = matmul(cold_piece, own_up)
    hot_gate = matmul(hot_piece, hot_gate_w)
    hot_up = matmul(hot_piece, hot_up_w)
    cold_part = matmul(swiglu(cold_gate, cold_up), own_down)
    hot_part = matmul(swiglu(hot_gate, hot_up), hot_down_w)
    model_width = cold_part.shape[1]
    came_back = lax.all_to_all(
        hot_part.reshape(experts, hot_rows, model_width),
        "expert",
        split_axis=0,
        concat_axis=0,
        tiled=True,
    )
    hot_part = lax.dynamic_index_in_dim(came_back, hot_id, 0, keepdims=False)
    returned = lax.all_to_all(
        cold_part.reshape(experts, capacity, model_width),
        "expert",
        split_axis=0,
        concat_axis=0,
        tiled=True,
    ).reshape(experts * capacity, model_width)
    assign_weight = route_share.reshape(2 * tok_rows) * is_live.astype(jnp.float32)
    cold_out = jnp.sum(
        (returned[target] * assign_weight[:, None]).reshape(tok_rows, 2, model_width), axis=1
    )
    hot_weight = jnp.sum(route_share * hot_match.astype(jnp.float32), axis=1)
    hot_out = hot_part[jnp.clip(hot_rank, 0, hot_rows - 1)] * hot_weight[:, None]
    mixed = lax.psum_scatter(cold_out + hot_out, "tensor", scatter_dimension=1, tiled=True).astype(
        jnp.bfloat16
    )
    expert_load = lax.psum(local_stats, "expert") / tok_rows
    return (mixed, expert_load)


def solution(mesh):
    placed = (
        P("expert", "tensor"),
        P("expert", None),
        P("expert", None),
        P("expert", None, "tensor"),
        P("expert", None, "tensor"),
        P("expert", "tensor", None),
    )

    def run(tokens, *rest):
        body = fused if fits(mesh, tokens) else local
        return jax.shard_map(
            body,
            mesh=mesh,
            in_specs=placed,
            out_specs=(P("expert", "tensor"), P()),
            check_vma=False,
        )(tokens, *rest)

    return run
```

profile of v0, /device:TPU:0, one launch (start us, length us, event | category | flops | bytes accessed | tf_op | source)
XLA Modules:
  0.0 38.0 jit_solution(17056873216701395699)
XLA Ops:
  0.6 34.8 %shard_map.77 = (bf16[48,384]{1,0:T(8,128)(2,1)}, f32[2,2]{1,0:T(2,128)}) custom-call(bf16[48,384]{1,0:T(8,128)(2,1)} %tok_ref.1, s32[2,48]{1,0:T(2,128)} %bitcast.2, s32[2,48]{1,0:T(2,128)} %bitcast.3, bf16[1,6144,512]{2,1,0:T(8,128)(2,1)} %gate_hbm.1, bf16[1,6144,512]{2,1,0:T(8,128)(2,1)} %up_hbm.1, bf16[1,512,6144]{2,1,0:T(8,128)(2,1)} %down_hbm.1), custom_call_target="tpu_custom_call" | custom-call | tf_op jit(solution)/shard_map/pallas_call | solution.py:296
  35.5 1.4 %copy.10 = bf16[48,384]{1,0:T(8,128)(2,1)} copy(bf16[48,384]{1,0:T(8,128)(2,1)} %get-tuple-element.4) | data formatting | bytes 73728
  36.8 1.2 %copy.11 = f32[2,2]{1,0:T(2,128)} copy(f32[2,2]{1,0:T(2,128)} %get-tuple-element.5) | data formatting | bytes 32
where the time goes:
time: 38.3 us; the launch traced here: 38 us
  Pallas kernels  34.8 us (91%)
  local copies, waits for them, and re-layouts  2.58 us (7%)
  between operations  0.64 us (2%)
    pallas_call x1, Pallas kernels, fused(): pl.pallas_call(functools.partial(kernel, depth), out_shape=(jax.ShapeDtyp...  34.8 us
    unnamed x2, local copies, waits for them, and re-layouts  2.58 us

commit v1 on v0

--- a/solution.py
+++ b/solution.py
@@ -285,6 +285,17 @@
         copy.wait_send()
 
 
+def put_out(mixed_ref, load_ref, mixed_out, load_out, sems):
+    copies = (
+        pltpu.make_async_copy(mixed_ref, mixed_out, sems.at[0]),
+        pltpu.make_async_copy(load_ref, load_out, sems.at[1]),
+    )
+    for copy in copies:
+        copy.start()
+    for copy in copies:
+        copy.wait()
+
+
 def fused(tokens, expert_ids, route_weight, gate_weight, up_weight, down_weight):
     groups, peers = lax.axis_size("expert"), lax.axis_size("tensor")
     rows, width = tokens.shape
@@ -293,11 +304,11 @@
     vmem = pl.BlockSpec(memory_space=pltpu.VMEM)
     anywhere = pl.BlockSpec(memory_space=pl.ANY)
     half, single, dma = jnp.bfloat16, jnp.float32, pltpu.SemaphoreType.DMA
-    return pl.pallas_call(
+    held = pl.pallas_call(
         functools.partial(kernel, depth),
         out_shape=(
-            jax.ShapeDtypeStruct((rows, width), half),
-            jax.ShapeDtypeStruct((2, groups), single),
+            pltpu.VMEM((rows, width), half),
+            pltpu.VMEM((2, groups), single),
         ),
         in_specs=[vmem, vmem, vmem, anywhere, anywhere, anywhere],
         out_specs=(vmem, vmem),
@@ -331,6 +342,17 @@
             collective_id=0, has_side_effects=True, vmem_limit_bytes=60 * 1024 * 1024
         ),
     )(tokens, expert_ids.T, route_weight.T, gate_weight, up_weight, down_weight)
+    held = [pltpu.with_memory_space_constraint(part, pltpu.VMEM) for part in held]
+    return pl.pallas_call(
+        put_out,
+        out_shape=(
+            jax.ShapeDtypeStruct((rows, width), half),
+            jax.ShapeDtypeStruct((2, groups), single),
+        ),
+        in_specs=[vmem, vmem],
+        out_specs=(pl.BlockSpec(memory_space=pltpu.HBM),) * 2,
+        scratch_shapes=[dma((2,))],
+    )(*held)
 
 
 def fits(mesh, tokens):

time: 38.3 us -> 35.6 us (0.930)
  local copies, waits for them, and re-layouts: 2.58 us -> 0 us
    unnamed x2 -> x0, local copies, waits for them, and re-layouts: 2.58 us -> none
    pallas_call x1 -> x2, Pallas kernels: 34.8 us -> 34.8 us  [the longest x1 34.2 us: fused(): pl.pallas_call(functools.partial(kernel, depth), out_shape=(pltpu.VMEM((r...]
where the time goes in v1:
time: 35.6 us; the launch traced here: 35.5 us
  Pallas kernels  34.8 us (98%)
  between operations  0.64 us (2%)
    pallas_call x1, Pallas kernels, fused(): pl.pallas_call(functools.partial(kernel, depth), out_shape=(pltpu.VMEM((r...  34.2 us

profile of v1, /device:TPU:0, one launch (start us, length us, event | category | flops | bytes accessed | tf_op | source)
XLA Modules:
  0.0 35.5 jit_solution(5021184570912077892)
XLA Ops:
  0.6 34.2 %shard_map.77 = (bf16[48,384]{1,0:T(8,128)(2,1)S(1)}, f32[2,2]{1,0:T(2,128)S(1)}) custom-call(bf16[48,384]{1,0:T(8,128)(2,1)} %tok_ref.1, s32[2,48]{1,0:T(2,128)} %bitcast.2, s32[2,48]{1,0:T(2,128)} %bitcast.3, bf16[1,6144,512]{2,1,0:T(8,128)(2,1)} %gate_hbm.1, bf16[1,6144,512]{2,1,0:T(8,128)(2,1)} %up_hbm.1, bf16[1,512,6144]{2,1,0:T(8,128)(2,1)} %down_hbm.1), custom_call_target="tpu_custom_call" | custom-call | tf_op jit(solution)/shard_map/pallas_call | solution.py:307
  34.8 0.6 %shard_map.78 = (bf16[48,384]{1,0:T(8,128)(2,1)}, f32[2,2]{1,0:T(2,128)}) custom-call(bf16[48,384]{1,0:T(8,128)(2,1)S(1)} %get-tuple-element.4.mixed_ref, f32[2,2]{1,0:T(2,128)S(1)} %get-tuple-element.5.load_ref), custom_call_target="tpu_custom_call" | custom-call | tf_op jit(solution)/shard_map/pallas_call | solution.py:346
